TPU v7x, 256 devices: a whole 4x4x8 slice. The times are simulated.
256 devices in a mesh: blk: 128 (over x, z, y_hi, core), rep: 2 (over y_lo).
Axes of the slice: x: 4, y: 4 (y_hi: 2, y_lo: 2; y = y_hi * 2 + y_lo), z: 8, core: 2. Of those that a mesh axis runs over, the one named last changes fastest.
Arguments:
- frames: bfloat16 [2, 6144, 384], P('rep', 'blk'), may hold values from -600 to 600
- codebook: bfloat16 [131072, 384], P('blk'), may hold values from -2 to 2
Outputs:
- log_total: float32 [2, 6144], P('rep', 'blk')
- counts: float32 [131072], P('blk')
- entropy: float32 [], replicated
All inputs are finite; a program needn't handle non-finite values.
Results may differ from a plain program's by a relative error of at most 0.00065.
Values may be sent and summed in bfloat16 or wider, within the bound.
No kernel may reach another device: no remote copies, remote signals or barrier semaphores. Data moves between devices by JAX's collectives and lax.ppermute only.
A program may use at most 128 MiB of HBM per device.

v0:
```python
import functools
import jax
import jax.numpy as jnp
from jax import lax
from jax.sharding import Mesh
from jax.sharding import PartitionSpec as P

BLK = ("blk_0", "blk_1", "blk_2", "blk_3")


def gathered_once(array, axis):
    leaves = jax.tree.leaves(array)
    sequence = sorted(range(len(leaves)), key=lambda k: -leaves[k].size)
    width = (1, *leaves[sequence[0]].shape)[-1]
    lines = [
        jnp.pad(leaves[k].reshape(-1), (0, -leaves[k].size % width)).reshape(-1, width)
        for k in sequence
    ]
    both, at, found = (lax.all_gather(jnp.concatenate(lines), axis), 0, {})
    for k, line in zip(sequence, lines):
        slab = both[:, at : at + len(line)].reshape(len(both), -1)
        found[k] = slab[:, : leaves[k].size].reshape(-1, *leaves[k].shape)
        at += len(line)
    numbers = iter(range(len(leaves)))
    return jax.tree.map(lambda _: found[next(numbers)], array)


def merged_by_axis(array, axes, combine):
    for axis in axes:
        pieces = gathered_once(array, axis)
        array = jax.tree.map(lambda part: part[0], pieces)
        for k in range(1, lax.axis_size(axis)):
            array = combine(array, jax.tree.map(lambda part: part[k], pieces))
    return array


def from_everyone(array, axis):
    copies = jnp.broadcast_to(array, (lax.axis_size(axis), *array.shape))
    return lax.all_to_all(copies, axis, split_axis=0, concat_axis=0, tiled=True)


def taken_together(array, axis):
    everything = from_everyone(array, axis)
    return jnp.sum(everything, axis=0)


def one_axis_at_a_time(array, axes):
    return functools.reduce(lax.psum, axes, array)


def score_block(moving, codebook):
    return lax.dot_general(
        moving, codebook, (((1,), (1,)), ((), ())), preferred_element_type=jnp.float32
    )


def merge_stats(earlier, later):
    new_high = jnp.maximum(earlier[0], later[0])
    new_total = earlier[1] * jnp.exp(earlier[0] - new_high) + later[1] * jnp.exp(
        later[0] - new_high
    )
    return (new_high, new_total)


def entropy_part(usage, frames_total):
    mean_use = usage / frames_total
    return -jnp.sum(mean_use * jnp.log(mean_use + 1e-07))


def per_device(frames, codebook):
    frame_rows = frames[0]
    shard_rows = frame_rows.shape[0]
    cycle_size = lax.axis_size(BLK)
    cycle_index = lax.axis_index(BLK)
    group_rows = shard_rows * cycle_size
    scores = score_block(lax.all_gather(frame_rows, BLK, axis=0, tiled=True), codebook)
    local_high = jnp.max(scores, axis=1)
    local_total = jnp.sum(jnp.exp(scores - local_high[:, None]), axis=1)
    row_high, row_total = merged_by_axis((local_high, local_total), BLK, merge_stats)
    lse_all = row_high + jnp.log(row_total)
    lse_own = lax.dynamic_slice_in_dim(lse_all, cycle_index * shard_rows, shard_rows, 0)
    usage_part = jnp.sum(jnp.exp(scores - lse_all[:, None]), axis=0)
    frames_total = group_rows * lax.axis_size("rep")
    usage = taken_together(usage_part, "rep")
    entropy = one_axis_at_a_time(entropy_part(usage, frames_total), BLK)
    return (lse_own[None, :], usage, entropy)


def solution(mesh):
    split = Mesh(
        mesh.devices.reshape(4, 8, 2, 2, mesh.shape["rep"]),
        ("blk_0", "blk_1", "blk_2", "blk_3", "rep"),
    )
    return jax.shard_map(
        per_device,
        mesh=split,
        in_specs=(P("rep", BLK, None), P(BLK, None)),
        out_specs=(P("rep", BLK), P(BLK), P()),
        check_vma=False,
    )
```

profile of v0, /device:TPU:1, one launch (start us, length us, event | category | flops | bytes accessed | tf_op | source)
XLA Modules:
  0.0 265.5 jit_solution(1867115252379620708)
XLA Ops:
  7.2 0.0 copy-start
  7.2 0.0 all-gather.11.cloned.1.call-start
  7.2 0.7 all-gather.11.cloned.1.call-update
  7.9 128.6 %all-gather.11.cloned.1.call-done = bf16[1,6144,384]{2,1,0:T(8,128)(2,1)} async-done(((bf16[1,48,384]{2,1,0:T(8,128)(2,1)}), bf16[1,6144,384]{2,1,0:T(8,128)(2,1)}) %all-gather.11.cloned.1.call-update) | async-done | bytes 4718608 | tf_op jit(solution)/shard_map/all_gather | solution.py:76
  136.5 0.0 copy-done
  136.5 14.0 %fusion.52 = (f32[6144]{0:T(1024)S(1)}, f32[6144,1024]{0,1:T(8,128)}) fusion(bf16[1024,384]{1,0:T(8,128)(2,1)S(1)} %copy-done, bf16[1,6144,384]{2,1,0:T(8,128)(2,1)} %all-gather.11.cloned.1.call-done), kind=kOutput, calls=%fused_computation.87 | convolution fusion | flops 4838123520 | bytes 30695424 | tf_op jit(solution)/shard_map/dot_general | solution.py:52
  150.5 0.0 copy-start.1
  150.5 10.4 %exponential_reduce_fusion.1 = f32[6144]{0:T(1024)S(1)} fusion(f32[6144,1024]{0,1:T(8,128)} %get-tuple-element.14, f32[6144]{0:T(1024)S(1)} %get-tuple-element.13), kind=kLoop, calls=%fused_computation.1 | loop fusion | flops 12576768 | bytes 25214976 | tf_op jit(solution)/shard_map/reduce_sum | solution.py:78
  161.0 10.2 %all-gather.5 = f32[4,2,6144]{2,1,0:T(2,128)S(1)} all-gather(f32[1,2,6144]{2,1,0:T(2,128)S(1)} %maximum_bitcast_fusion), channel_id=3, replica_groups=mesh['blk_0'=4,'blk_1'=8,'blk_2'=2,'blk_3'=2,'rep'=2] {'blk_0'}, dimensions={0}, use_global_device_ids=true | all-gather | bytes 245760 | tf_op jit(solution)/shard_map/all_gather | solution.py:19
  171.1 0.2 fusion.27
  171.4 19.0 %all-gather.6 = f32[8,2,6144]{2,1,0:T(2,128)S(1)} all-gather(f32[1,2,6144]{2,1,0:T(2,128)S(1)} %maximum_bitcast_fusion.1), channel_id=4, replica_groups=mesh['blk_0'=4,'blk_1'=8,'blk_2'=2,'blk_3'=2,'rep'=2] {'blk_1'}, dimensions={0}, use_global_device_ids=true | all-gather | bytes 442368 | tf_op jit(solution)/shard_map/all_gather | solution.py:19
  190.5 0.6 fusion.6
  191.1 5.1 %all-gather.7 = f32[2,2,6144]{2,1,0:T(2,128)S(1)} all-gather(f32[1,2,6144]{2,1,0:T(2,128)S(1)} %maximum_bitcast_fusion.2), channel_id=5, replica_groups=mesh['blk_0'=4,'blk_1'=8,'blk_2'=2,'blk_3'=2,'rep'=2] {'blk_2'}, dimensions={0}, use_global_device_ids=true | all-gather | bytes 147456 | tf_op jit(solution)/shard_map/all_gather | solution.py:19
  196.2 0.1 fusion.3
  196.4 11.4 %all-gather.8 = f32[2,2,6144]{2,1,0:T(2,128)S(1)} all-gather(f32[1,2,6144]{2,1,0:T(2,128)S(1)} %maximum_bitcast_fusion.3), channel_id=6, replica_groups=mesh['blk_0'=4,'blk_1'=8,'blk_2'=2,'blk_3'=2,'rep'=2] {'blk_3'}, dimensions={0}, use_global_device_ids=true | all-gather | bytes 147456 | tf_op jit(solution)/shard_map/all_gather | solution.py:19
  207.8 0.1 fusion.51
  207.9 0.0 copy-done.1
  207.9 3.8 %exponential_reduce_fusion = f32[1024]{0:T(1024)S(1)} fusion(f32[6144,1024]{0,1:T(8,128)S(1)} %copy-done.1, f32[6144]{0:T(1024)S(1)} %log_add_fusion), kind=kLoop, calls=%fused_computation | loop fusion | flops 12581888 | bytes 25194496 | tf_op jit(solution)/shard_map/reduce_sum | solution.py:82
  211.7 0.6 broadcast_in_dim.9
  212.3 3.2 %all-to-all-start = ((f32[2,1,1024]{2,1,0:T(1,128)}), f32[2,1,1024]{2,1,0:T(1,128)S(1)}, u32[]{:S(2)}, u32[]{:S(2)}) async-start(f32[2,1,1024]{2,1,0:T(1,128)} %broadcast_in_dim.9), calls=%async_computation | async-start | bytes 16384 | tf_op jit(solution)/shard_map/all_to_all | solution.py:39
  215.6 2.6 all-to-all-done
  218.2 0.0 copy-start.2
  218.3 0.6 multiply_reduce_fusion
  219.5 8.9 %psum.28 = f32[]{:T(128)} all-reduce(f32[]{:T(128)S(6)} %neg.3), channel_id=1, replica_groups=mesh['blk_0'=4,'blk_1'=8,'blk_2'=2,'blk_3'=2,'rep'=2] {'blk_0'}, use_global_device_ids=true, to_apply=%region_5.6 | all-reduce | flops 1 | bytes 8 | tf_op jit(solution)/shard_map/psum | solution.py:48
  228.5 12.5 %psum.29 = f32[]{:T(128)} all-reduce(f32[]{:T(128)} %psum.28), channel_id=1, replica_groups=mesh['blk_0'=4,'blk_1'=8,'blk_2'=2,'blk_3'=2,'rep'=2] {'blk_1'}, use_global_device_ids=true, to_apply=%region_6.7 | all-reduce | flops 1 | bytes 8 | tf_op jit(solution)/shard_map/psum | solution.py:48
  241.0 5.9 %psum.30 = f32[]{:T(128)} all-reduce(f32[]{:T(128)} %psum.29), channel_id=1, replica_groups=mesh['blk_0'=4,'blk_1'=8,'blk_2'=2,'blk_3'=2,'rep'=2] {'blk_2'}, use_global_device_ids=true, to_apply=%region_7.8 | all-reduce | flops 1 | bytes 8 | tf_op jit(solution)/shard_map/psum | solution.py:48
  246.9 0.6 dynamic-slice_bitcast_fusion
  247.5 11.2 %psum.31 = f32[]{:T(128)} all-reduce(f32[]{:T(128)} %psum.30), channel_id=1, replica_groups=mesh['blk_0'=4,'blk_1'=8,'blk_2'=2,'blk_3'=2,'rep'=2] {'blk_3'}, use_global_device_ids=true, to_apply=%region_8.9 | all-reduce | flops 1 | bytes 8 | tf_op jit(solution)/shard_map/psum | solution.py:48
  258.6 0.0 copy-done.2
  (6 shorter events, 0.2 us)
Async XLA Ops:
  7.2 129.3 %copy-start = (bf16[1024,384]{1,0:T(8,128)(2,1)S(1)}, bf16[1024,384]{1,0:T(8,128)(2,1)}, u32[]{:S(2)}) copy-start(bf16[1024,384]{1,0:T(8,128)(2,1)} %param.3) | copy-start | bytes 2359300
  7.2 129.3 %all-gather.11.cloned.1.call-start = ((), (), s32[]{:S(2)}) async-start(), calls=%async_computation.1 | async-start | bytes 4755456 | tf_op jit(solution)/shard_map/all_gather | solution.py:76
  150.5 57.4 %copy-start.1 = (f32[6144,1024]{0,1:T(8,128)S(1)}, f32[6144,1024]{0,1:T(8,128)}, u32[]{:S(2)}) copy-start(f32[6144,1024]{0,1:T(8,128)} %get-tuple-element.14) | copy-start | bytes 75497472
  212.3 5.9 %all-to-all-start = ((f32[2,1,1024]{2,1,0:T(1,128)}), f32[2,1,1024]{2,1,0:T(1,128)S(1)}, u32[]{:S(2)}, u32[]{:S(2)}) async-start(f32[2,1,1024]{2,1,0:T(1,128)} %broadcast_in_dim.9), calls=%async_computation | async-start | bytes 16384 | tf_op jit(solution)/shard_map/all_to_all | solution.py:39
  218.2 40.4 %copy-start.2 = (f32[1024]{0:T(1024)}, f32[1024]{0:T(1024)S(1)}, u32[]{:S(2)}) copy-start(f32[1024]{0:T(1024)S(1)} %reduce_sum.38) | copy-start | bytes 12292
Sparse Core Ops, SparseCore 0:
  11.9 124.5 all-gather.10
where the time goes:
time: 266 us; the launch traced here: 265 us
  waiting for transfers between devices  132 us (50%)
  blocking collectives  84.3 us (32%)
  other arithmetic  16 us (6%)
  between operations  14.8 us (6%)
  matrix products  14 us (5%)
  starting transfers between devices  3.26 us (1%)
    all_gather x1, waiting for transfers between devices, per_device(): lax.all_gather(frame_rows, BLK, axis=0, tiled=True)  129 us
    all_gather x4, blocking collectives, gathered_once(): both, at, found = (lax.all_gather(jnp.concatenate(lines), axis), 0, {})  45.7 us
    psum x4, blocking collectives, one_axis_at_a_time(): return functools.reduce(lax.psum, axes, array)  38.5 us
    dot_general x1, matrix products, score_block(): lax.dot_general(moving, codebook, (((1,), (1,)), ((), ())), preferred_ele...  14 us
    reduce_sum x1, other arithmetic, per_device(): local_total = jnp.sum(jnp.exp(scores - local_high[:, None]), axis=1)  10.4 us
  transfers between devices with their start and end apart: 2, of which 2 were waited for; matrix products, arithmetic and copies ran while one was open for 0% of the time, Pallas kernels for 0%

commit v1 on v0

--- a/solution.py
+++ b/solution.py
@@ -73,7 +73,12 @@
     cycle_size = lax.axis_size(BLK)
     cycle_index = lax.axis_index(BLK)
     group_rows = shard_rows * cycle_size
-    scores = score_block(lax.all_gather(frame_rows, BLK, axis=0, tiled=True), codebook)
+    scores = score_block(
+        jnp.concatenate(
+            lax.all_to_all(jnp.stack([frame_rows] * lax.axis_size(BLK)), BLK, 0, 0), axis=0
+        ),
+        codebook,
+    )
     local_high = jnp.max(scores, axis=1)
     local_total = jnp.sum(jnp.exp(scores - local_high[:, None]), axis=1)
     row_high, row_total = merged_by_axis((local_high, local_total), BLK, merge_stats)

time: 266 us -> 247 us (0.929)
  waiting for transfers between devices: 132 us -> 2.64 us
  blocking collectives: 84.3 us -> 209 us
  between operations: 14.8 us -> 1.39 us
    all_gather x1 -> x0, waiting for transfers between devices: 129 us -> none  [per_device(): lax.all_gather(frame_rows, BLK, axis=0, tiled=True)]
    all_to_all x0 -> x1, blocking collectives: none -> 126 us  [per_device(): lax.all_to_all(jnp.stack([frame_rows] * lax.axis_size(BLK)), BLK, 0, 0)]
  transfers between devices with their start and end apart: 2 -> 1, of which waited for: 2 -> 1; matrix products, arithmetic and copies ran while one was open for 0% -> 0% of each run, Pallas kernels for 0% -> 0%
where the time goes in v1:
time: 247 us
  blocking collectives  209 us (85%)
  other arithmetic  16 us (6%)
  matrix products  11.8 us (5%)
  starting transfers between devices  3.22 us (1%)
  waiting for transfers between devices  2.64 us (1%)
  local copies, waits for them, and re-layouts  2.53 us (1%)
    all_to_all x1, blocking collectives, per_device(): lax.all_to_all(jnp.stack([frame_rows] * lax.axis_size(BLK)), BLK, 0, 0)  126 us
    all_gather x4, blocking collectives, gathered_once(): both, at, found = (lax.all_gather(jnp.concatenate(lines), axis), 0, {})  45.5 us
    psum x4, blocking collectives, one_axis_at_a_time(): return functools.reduce(lax.psum, axes, array)  37.3 us
    dot_general x1, matrix products, score_block(): lax.dot_general(moving, codebook, (((1,), (1,)), ((), ())), preferred_ele...  11.8 us
    reduce_sum x1, other arithmetic, per_device(): local_total = jnp.sum(jnp.exp(scores - local_high[:, None]), axis=1)  10.4 us
  transfers between devices with their start and end apart: 1, of which 1 were waited for; matrix products, arithmetic and copies ran while one was open for 0% of the time, Pallas kernels for 0%

profile of v1, /device:TPU:1, one launch (start us, length us, event | category | flops | bytes accessed | tf_op | source)
XLA Modules:
  0.0 246.8 jit_solution(9040524913679452634)
XLA Ops:
  0.6 0.0 copy-start
  0.6 1.2 stack.3
  1.9 126.3 %all_to_all.11 = bf16[128,48,384]{2,1,0:T(8,128)(2,1)S(1)} all-to-all(bf16[128,48,384]{2,1,0:T(8,128)(2,1)S(1)} %stack.3), channel_id=1, replica_groups=mesh['blk_0'=4,'blk_1'=8,'blk_2'=2,'blk_3'=2,'rep'=2] {'blk_0','blk_1','..., dimensions={0} | all-to-all | bytes 9437184 | tf_op jit(solution)/shard_map/all_to_all | solution.py:78
  128.2 0.0 copy-done
  128.2 11.8 %fusion.50 = (f32[6144]{0:T(1024)S(1)}, f32[6144,1024]{0,1:T(8,128)}) fusion(bf16[6144,384]{1,0:T(8,128)(2,1)S(1)} %bitcast.274, bf16[1024,384]{1,0:T(8,128)(2,1)S(1)} %copy-done), kind=kOutput, calls=%fused_computation.85 | convolution fusion | flops 4838123520 | bytes 30695424 | tf_op jit(solution)/shard_map/dot_general | solution.py:52
  140.1 0.0 copy-start.1
  140.1 10.4 %exponential_reduce_fusion.1 = f32[6144]{0:T(1024)S(1)} fusion(f32[6144,1024]{0,1:T(8,128)} %get-tuple-element.14, f32[6144]{0:T(1024)S(1)} %get-tuple-element.13), kind=kLoop, calls=%fused_computation.1 | loop fusion | flops 12576768 | bytes 25214976 | tf_op jit(solution)/shard_map/reduce_sum | solution.py:83
  150.5 9.4 %all-gather.4 = f32[4,2,6144]{2,1,0:T(2,128)S(1)} all-gather(f32[1,2,6144]{2,1,0:T(2,128)S(1)} %maximum_bitcast_fusion), channel_id=2, replica_groups=mesh['blk_0'=4,'blk_1'=8,'blk_2'=2,'blk_3'=2,'rep'=2] {'blk_0'}, dimensions={0}, use_global_device_ids=true | all-gather | bytes 245760 | tf_op jit(solution)/shard_map/all_gather | solution.py:19
  159.9 0.2 fusion.25
  160.2 19.4 %all-gather.5 = f32[8,2,6144]{2,1,0:T(2,128)S(1)} all-gather(f32[1,2,6144]{2,1,0:T(2,128)S(1)} %maximum_bitcast_fusion.1), channel_id=3, replica_groups=mesh['blk_0'=4,'blk_1'=8,'blk_2'=2,'blk_3'=2,'rep'=2] {'blk_1'}, dimensions={0}, use_global_device_ids=true | all-gather | bytes 442368 | tf_op jit(solution)/shard_map/all_gather | solution.py:19
  179.6 0.6 fusion.4
  180.2 5.1 %all-gather.6 = f32[2,2,6144]{2,1,0:T(2,128)S(1)} all-gather(f32[1,2,6144]{2,1,0:T(2,128)S(1)} %maximum_bitcast_fusion.2), channel_id=4, replica_groups=mesh['blk_0'=4,'blk_1'=8,'blk_2'=2,'blk_3'=2,'rep'=2] {'blk_2'}, dimensions={0}, use_global_device_ids=true | all-gather | bytes 147456 | tf_op jit(solution)/shard_map/all_gather | solution.py:19
  185.3 0.1 fusion.1
  185.5 11.6 %all-gather.7 = f32[2,2,6144]{2,1,0:T(2,128)S(1)} all-gather(f32[1,2,6144]{2,1,0:T(2,128)S(1)} %maximum_bitcast_fusion.3), channel_id=5, replica_groups=mesh['blk_0'=4,'blk_1'=8,'blk_2'=2,'blk_3'=2,'rep'=2] {'blk_3'}, dimensions={0}, use_global_device_ids=true | all-gather | bytes 147456 | tf_op jit(solution)/shard_map/all_gather | solution.py:19
  197.1 0.1 fusion.49
  197.2 0.0 copy-done.1
  197.2 3.8 %exponential_reduce_fusion = f32[1024]{0:T(1024)S(1)} fusion(f32[6144,1024]{0,1:T(8,128)S(1)} %copy-done.1, f32[6144]{0:T(1024)S(1)} %log_add_fusion), kind=kLoop, calls=%fused_computation | loop fusion | flops 12581888 | bytes 25194496 | tf_op jit(solution)/shard_map/reduce_sum | solution.py:87
  201.1 0.6 broadcast_in_dim.9
  201.7 3.2 %all-to-all-start.1 = ((f32[2,1,1024]{2,1,0:T(1,128)}), f32[2,1,1024]{2,1,0:T(1,128)S(1)}, u32[]{:S(2)}, u32[]{:S(2)}) async-start(f32[2,1,1024]{2,1,0:T(1,128)} %broadcast_in_dim.9), calls=%async_computation.1 | async-start | bytes 16384 | tf_op jit(solution)/shard_map/all_to_all | solution.py:39
  204.9 2.6 %all-to-all-done.1 = f32[2,1,1024]{2,1,0:T(1,128)S(1)} async-done(((f32[2,1,1024]{2,1,0:T(1,128)}), f32[2,1,1024]{2,1,0:T(1,128)S(1)}, u32[]{:S(2)}, u32[]{:S(2)}) %all-to-all-start.1) | async-done | bytes 8224 | tf_op jit(solution)/shard_map/all_to_all | solution.py:39
  207.6 0.0 copy-start.2
  207.6 0.6 multiply_reduce_fusion
  208.8 7.3 %psum.28 = f32[]{:T(128)} all-reduce(f32[]{:T(128)S(6)} %neg.3), channel_id=1, replica_groups=mesh['blk_0'=4,'blk_1'=8,'blk_2'=2,'blk_3'=2,'rep'=2] {'blk_0'}, use_global_device_ids=true, to_apply=%region_5.6 | all-reduce | flops 1 | bytes 8 | tf_op jit(solution)/shard_map/psum | solution.py:48
  216.1 13.0 %psum.29 = f32[]{:T(128)} all-reduce(f32[]{:T(128)} %psum.28), channel_id=1, replica_groups=mesh['blk_0'=4,'blk_1'=8,'blk_2'=2,'blk_3'=2,'rep'=2] {'blk_1'}, use_global_device_ids=true, to_apply=%region_6.7 | all-reduce | flops 1 | bytes 8 | tf_op jit(solution)/shard_map/psum | solution.py:48
  229.1 5.9 %psum.30 = f32[]{:T(128)} all-reduce(f32[]{:T(128)} %psum.29), channel_id=1, replica_groups=mesh['blk_0'=4,'blk_1'=8,'blk_2'=2,'blk_3'=2,'rep'=2] {'blk_2'}, use_global_device_ids=true, to_apply=%region_7.8 | all-reduce | flops 1 | bytes 8 | tf_op jit(solution)/shard_map/psum | solution.py:48
  235.0 0.6 dynamic-slice_bitcast_fusion
  235.6 11.2 %psum.31 = f32[]{:T(128)} all-reduce(f32[]{:T(128)} %psum.30), channel_id=1, replica_groups=mesh['blk_0'=4,'blk_1'=8,'blk_2'=2,'blk_3'=2,'rep'=2] {'blk_3'}, use_global_device_ids=true, to_apply=%region_8.9 | all-reduce | flops 1 | bytes 8 | tf_op jit(solution)/shard_map/psum | solution.py:48
  246.8 0.0 copy-done.2
  (6 shorter events, 0.2 us)
Async XLA Ops:
  0.6 127.6 %copy-start = (bf16[1024,384]{1,0:T(8,128)(2,1)S(1)}, bf16[1024,384]{1,0:T(8,128)(2,1)}, u32[]{:S(2)}) copy-start(bf16[1024,384]{1,0:T(8,128)(2,1)} %param.3) | copy-start | bytes 2359300
  140.1 57.2 %copy-start.1 = (f32[6144,1024]{0,1:T(8,128)S(1)}, f32[6144,1024]{0,1:T(8,128)}, u32[]{:S(2)}) copy-start(f32[6144,1024]{0,1:T(8,128)} %get-tuple-element.14) | copy-start | bytes 75497472
  201.7 5.9 %all-to-all-start.1 = ((f32[2,1,1024]{2,1,0:T(1,128)}), f32[2,1,1024]{2,1,0:T(1,128)S(1)}, u32[]{:S(2)}, u32[]{:S(2)}) async-start(f32[2,1,1024]{2,1,0:T(1,128)} %broadcast_in_dim.9), calls=%async_computation.1 | async-start | bytes 16384 | tf_op jit(solution)/shard_map/all_to_all | solution.py:39
  207.6 39.2 %copy-start.2 = (f32[1024]{0:T(1024)}, f32[1024]{0:T(1024)S(1)}, u32[]{:S(2)}) copy-start(f32[1024]{0:T(1024)S(1)} %reduce_sum.38) | copy-start | bytes 12292
